TPU v7x, 32 devices: a whole 2x2x4 slice. The times are simulated.
32 devices in a mesh: win: 4 (over y, core), tile: 8 (over z, x).
Axes of the slice: x: 2, y: 2, z: 4, core: 2. Of those that a mesh axis runs over, the one named last changes fastest.
Arguments:
- state: float32 [4, 8, 5, 32, 8, 128], P('win', 'tile'), may hold values from -6 to 6
- obs_weight: float32 [4, 8, 5, 32, 8, 128], P('win', 'tile'), may hold values from 0 to 1
- trajectory: bfloat16 [4, 8, 3, 2, 32, 8, 128], P('win', 'tile'), may hold values from -0.8984375 to 0.8984375
- coupling: float32 [5, 5], replicated, may hold values from -0.9 to 0.9
- prec_scale: float32 [5, 32], replicated, may hold values from 0.5 to 2
Outputs:
- hess_vec: float32 [4, 8, 5, 32, 8, 128], P('win', 'tile')
All inputs are finite; a program needn't handle non-finite values.
Results may differ from a plain program's by a relative error of at most 0.0003.
Values sent between devices are 32-bit elements; how exact they have to be, the bound alone decides.
A program may use at most 64 MiB of HBM per device.

v0:
```python
import functools

import jax
import jax.numpy as jnp
from jax import lax
from jax.experimental import pallas as pl
from jax.experimental.pallas import tpu as pltpu
from jax.sharding import PartitionSpec as P

TY = 4
GROUP = 8

smooth_weight = 0.2


def kernel(windows, tiles, keep, state, obs, winds, coupling, prec, out,
           nat, onat, wnat, cs, ps, fld, wr, arrived, wgt, gf, ret, xs, xr, ys, yr,
           load, hsend, hrecv, wsend, wrecv, msend, mrecv):
    steps, groups, cx, cy = wr.shape[0] // 2, wr.shape[1], wr.shape[2], wr.shape[4]
    variables = fld.shape[1]
    span = GROUP * cx
    end = windows - 1
    moved, edge, back0 = steps, steps + 1, steps + 2
    helping = keep < groups
    k = lax.axis_index("win")
    t = lax.axis_index("tile")
    before_x, after_x = lax.rem(t + tiles - TY, tiles), lax.rem(t + TY, tiles)
    before_y, after_y = lax.rem(t + tiles - 1, tiles), lax.rem(t + 1, tiles)
    around = (before_x, after_x, before_y, after_y)
    is_first, is_last = k == 0, k == end
    lo, hi = jnp.where(is_last, keep, 0), jnp.where(is_first, keep, groups)
    sel = jnp.where(is_last, 1, 0)
    nxt = jnp.where(is_last, 1, k + 1)
    edges = jnp.where(is_last, edge, 0)

    def when(cond):
        return pl.when(cond)

    def part(g):
        return pl.ds(pl.multiple_of(g * span, span), span)

    def state_in(g):
        return pltpu.make_async_copy(state.at[:, part(g)], nat.at[:, part(g)], load.at[g])

    def winds_in(n):
        return pltpu.make_async_copy(winds.at[pl.ds(2 * n, 2)], wnat.at[pl.ds(2 * n, 2)], load.at[groups + n])

    obs_in = pltpu.make_async_copy(obs, onat, load.at[groups + steps])
    prec_in = pltpu.make_async_copy(prec, ps, load.at[groups + steps + 1])
    coupling_in = pltpu.make_async_copy(coupling, cs, load.at[groups + steps + 2])

    order = tuple(range(keep, groups)) + tuple(range(keep))
    for g in order:
        state_in(g).start()
    coupling_in.start()

    @when(~is_last)
    def _():
        for n in range(steps):
            winds_in(n).start()
    prec_in.start()
    obs_in.start()

    barrier = pltpu.get_barrier_semaphore()

    def greet(win, others):
        pl.semaphore_signal(barrier, inc=1, device_id={"win": win})
        for other in others:
            pl.semaphore_signal(barrier, inc=1, device_id={"win": win, "tile": other})
        return

    for other in around:
        pl.semaphore_signal(barrier, inc=1, device_id={"tile": other})

    @when(k < end)
    def _():
        greet(k + 1, around)

    @when(k > 0)
    def _():
        greet(k - 1, around)

    met = 4 + 5 * jnp.where(k < end, 1, 0) + 5 * jnp.where(k > 0, 1, 0)
    if helping:
        @when(is_first)
        def _():
            greet(end, ())

        @when(k == 1)
        def _():
            greet(end, around)

        @when(is_last)
        def _():
            greet(0, ())
            greet(1, around)
        met = met + jnp.where(is_first, 1, 0) + 5 * jnp.where(k == 1, 1, 0) + 6 * jnp.where(is_last, 1, 0)

    shape = (GROUP, cy)
    lane = lax.broadcasted_iota(jnp.int32, shape, 1)
    level = lax.broadcasted_iota(jnp.int32, shape, 0)
    pair, odd = lane // 2, lane % 2 == 1
    at_start, at_end = lane == 0, lane == cy - 1

    def halo(slot, g, win, low, high):
        made = []
        for side, to in enumerate((before_y, after_y)):
            made.append(pltpu.make_async_remote_copy(
                src_ref=ys.at[slot, g], dst_ref=yr.at[slot, side, g],
                send_sem=hsend.at[slot, side, g], recv_sem=hrecv.at[slot, side, g],
                device_id={"win": win, "tile": to}))
        for side, (to, rows) in enumerate(((before_x, low), (after_x, high))):
            made.append(pltpu.make_async_remote_copy(
                src_ref=rows, dst_ref=xr.at[slot, side, g],
                send_sem=hsend.at[slot, 2 + side, g], recv_sem=hrecv.at[slot, 2 + side, g],
                device_id={"win": win, "tile": to}))
        return made

    def field_halo(slot, g, win, index):
        return halo(slot, g, win, fld.at[index, :, g, 0], fld.at[index, :, g, cx - 1])

    def flux_halo(slot, g):
        return halo(slot, g, k, xs.at[slot - back0, 0, g], xs.at[slot - back0, 1, g])

    def receive(slot, g):
        for copy in halo(slot, g, k, xr.at[slot, 0, g], xr.at[slot, 1, g]):
            copy.wait_recv()

    def onward(g):
        return pltpu.make_async_remote_copy(
            src_ref=fld.at[steps + 1, :, g], dst_ref=arrived.at[:, g],
            send_sem=wsend.at[0, g], recv_sem=wrecv.at[0, g], device_id={"win": nxt})

    def back(g):
        source = jnp.where(k == 1, jnp.where(g < keep, 0, end), k - 1)
        return pltpu.make_async_remote_copy(
            src_ref=wgt.at[0, :, g], dst_ref=gf.at[0, :, g],
            send_sem=wsend.at[1, g], recv_sem=wrecv.at[1, g], device_id={"win": source})

    def lend_state(g):
        return pltpu.make_async_remote_copy(
            src_ref=fld.at[0, :, g], dst_ref=fld.at[1, :, g],
            send_sem=msend.at[0, g], recv_sem=mrecv.at[0, g], device_id={"win": end})

    def lend_winds(n, g):
        return pltpu.make_async_remote_copy(
            src_ref=wr.at[pl.ds(2 * n, 2), g], dst_ref=wr.at[pl.ds(2 * n, 2), g],
            send_sem=msend.at[2 + n, g], recv_sem=mrecv.at[2 + n, g], device_id={"win": end})

    def give_back(g):
        return pltpu.make_async_remote_copy(
            src_ref=ret.at[:, g], dst_ref=ret.at[:, g],
            send_sem=msend.at[1, g], recv_sem=mrecv.at[1, g], device_id={"win": 0})

    def place(v, r):
        return v * cx + r

    def pack(packed, value, v, r):
        p = place(v, r)
        return jnp.where(pair == p, pltpu.roll(value, 2 * p + 1, 1), packed)

    def rims(north, south):
        return jnp.where(odd, north, pltpu.roll(south, 2, 1))

    def sides(value, rim, v, r):
        edge_pair = pltpu.roll(rim, cy - 2 - 2 * place(v, r), 1)
        north = jnp.where(at_end, edge_pair, pltpu.roll(value, cy - 1, 1))
        south = jnp.where(at_start, edge_pair, pltpu.roll(value, 1, 1))
        return north, south

    def every(f):
        for v in range(variables):
            f(v)

    def rows_of(g, r):
        return pl.ds(g * span + r, GROUP, stride=cx)

    def convert_state(g):
        for v in range(variables):
            for r in range(cx):
                fld[0, v, g, r] = nat[v, rows_of(g, r), :]

    def pack_state(g, index, slot):
        packed = jnp.zeros(shape, jnp.float32)
        for v in range(variables):
            for r in range(cx):
                packed = pack(packed, fld[index, v, g, r], v, r)
        ys[slot, g] = packed

    def over(a, b, f):
        lax.fori_loop(a, b, lambda g, c: (f(g), c)[1], 0)

    for g in order:
        state_in(g).wait()
        convert_state(g)
        if g == order[0]:
            pl.semaphore_wait(barrier, met)
        if g >= keep:
            @when(is_first)
            def _():
                lend_state(g).start()

        @when((k < end) & (g < hi))
        def _():
            pack_state(g, 0, 0)
            for copy in field_halo(0, g, k, 0):
                copy.start()

    def convert_winds(n, g):
        for way in range(2):
            for j in range(GROUP):
                tile = wnat[2 * n + way, g * GROUP + j].astype(jnp.float32)
                for r in range(cx):
                    wr[2 * n + way, g, r, pl.ds(j, 1), :] = tile[r:r + 1]

    @when(k < end)
    def _():
        for n in range(steps):
            winds_in(n).wait()

            def one(i, n=n):
                g = lax.rem(i + keep, groups)
                convert_winds(n, g)
                if helping:
                    @when(is_first & (g >= keep))
                    def _():
                        lend_winds(n, g).start()
            over(0, groups, one)

    coupling_in.wait()

    if helping:
        @when(is_last)
        def _():
            @functools.partial(over, keep, groups)
            def _(g):
                lend_state(g).wait_recv()
                pack_state(g, 1, 0)
                for copy in field_halo(0, g, k, 1):
                    copy.start()

    @when(is_last)
    def _():
        @functools.partial(over, 0, groups)
        def _(g):
            pack_state(g, 0, edge)
            for copy in field_halo(edge, g, k, 0):
                copy.start()

    def forward(n, g):
        if helping:
            @when(is_last)
            def _():
                lend_winds(n, g).wait_recv()
        receive(n, g)
        source = jnp.where(n == 0, sel, n + 1)
        rim = rims(yr[n, 0, g], yr[n, 1, g])

        def row(r):
            if r < 0:
                return [xr[n, 1, g, v] for v in range(variables)]
            if r == cx:
                return [xr[n, 0, g, v] for v in range(variables)]
            return [fld[source, v, g, r] for v in range(variables)]

        west, here = row(-1), row(0)
        packed = jnp.zeros(shape, jnp.float32)
        for r in range(cx):
            east = row(r + 1)
            u, w = wr[2 * n, g, r], wr[2 * n + 1, g, r]
            for v in range(variables):
                north, south = sides(here[v], rim, v, r)
                total = here[v] + u * (east[v] - west[v]) + w * (north - south)
                for b in range(variables):
                    total = total + cs[v, b] * here[b]
                fld[n + 2, v, g, r] = total
                packed = pack(packed, total, v, r)
            west, here = here, east
        ys[n + 1, g] = packed
        ends = n == steps - 1
        for copy in field_halo(n + 1, g, jnp.where(ends, nxt, k), n + 2):
            copy.start()

        @when(ends)
        def _():
            onward(g).start()

    @functools.partial(over, 0, steps)
    def _(n):
        over(lo, hi, lambda g: forward(n, g))

    prec_in.wait()

    def stencil(g, row, rim, index):
        scale = []
        for v in range(variables):
            s = jnp.zeros(shape, jnp.float32)
            for j in range(GROUP):
                s = jnp.where(level == j, ps[v, g * GROUP + j], s)
            scale.append(s)
        west, here = row(-1), row(0)
        for r in range(cx):
            east = row(r + 1)
            for v in range(variables):
                north, south = sides(here[v], rim, v, r)
                smooth = (1.0 + 4.0 * smooth_weight) * here[v] - smooth_weight * (
                    east[v] + west[v] + north + south)
                wgt[index, v, g, r] = scale[v] * smooth
            west, here = here, east

    def start_window(g):
        def row(r):
            if r < 0:
                return [xr[0, 1, g, v] for v in range(variables)]
            if r == cx:
                return [xr[0, 0, g, v] for v in range(variables)]
            return [fld[sel, v, g, r] for v in range(variables)]
        stencil(g, row, rims(yr[0, 0, g], yr[0, 1, g]), sel)

    def mismatch(g):
        @when(is_last)
        def _():
            receive(edge, g)
        receive(moved, g)
        onward(g).wait_recv()

        def row(r):
            if r < 0:
                return [xr[edges, 1, g, v] - xr[moved, 1, g, v] for v in range(variables)]
            if r == cx:
                return [xr[edges, 0, g, v] - xr[moved, 0, g, v] for v in range(variables)]
            return [fld[0, v, g, r] - arrived[v, g, r] for v in range(variables)]
        stencil(g, row, rims(yr[edges, 0, g] - yr[moved, 0, g], yr[edges, 1, g] - yr[moved, 1, g]), 0)
        back(g).start()

    @when(k > 0)
    def _():
        over(0, groups, mismatch)

    @when(is_first | is_last)
    def _():
        over(lo, hi, start_window)

    def begin_back(g):
        back(g).wait_recv()
        n = steps - 1
        packed = jnp.zeros(shape, jnp.float32)
        for r in range(cx):
            u, w = wr[2 * n, g, r], wr[2 * n + 1, g, r]
            for v in range(variables):
                value = gf[0, v, g, r]
                if r == 0:
                    xs[0, 0, g, v] = u * value
                if r == cx - 1:
                    xs[0, 1, g, v] = u * value
                packed = pack(packed, w * value, v, r)
        ys[back0, g] = packed
        for copy in flux_halo(back0, g):
            copy.start()

    def backward(i, g, final):
        n = steps - 1 - i
        slot = back0 + i
        receive(slot, g)
        rim = rims(yr[slot, 0, g], yr[slot, 1, g])

        def row(r):
            if r < 0:
                return None, [xr[slot, 1, g, v] for v in range(variables)]
            if r == cx:
                return None, [xr[slot, 0, g, v] for v in range(variables)]
            u = wr[2 * n, g, r]
            values = [gf[i, v, g, r] for v in range(variables)]
            return values, [u * value for value in values]

        (_, west), (values, here) = row(-1), row(0)
        packed = jnp.zeros(shape, jnp.float32)
        for r in range(cx):
            values_east, east = row(r + 1)
            w = wr[2 * n + 1, g, r]
            if not final:
                u_next, w_next = wr[2 * n - 2, g, r], wr[2 * n - 1, g, r]
            for v in range(variables):
                north, south = sides(w * values[v], rim, v, r)
                total = values[v] + (west[v] - east[v]) + (south - north)
                for b in range(variables):
                    total = total + cs[b, v] * values[b]
                if final:
                    ret[v, g, r] = wgt[sel, v, g, r] - total
                    continue
                gf[i + 1, v, g, r] = total
                if r == 0:
                    xs[i + 1, 0, g, v] = u_next * total
                if r == cx - 1:
                    xs[i + 1, 1, g, v] = u_next * total
                packed = pack(packed, w_next * total, v, r)
            west, values, here = here, values_east, east
        if not final:
            ys[slot + 1, g] = packed
            for copy in flux_halo(slot + 1, g):
                copy.start()

    over(lo, hi, begin_back)

    @functools.partial(over, 0, steps - 1)
    def _(i):
        over(lo, hi, lambda g: backward(i, g, False))

    obs_in.wait()

    def finish(g, term):
        for v in range(variables):
            for r in range(cx):
                rows = rows_of(g, r)
                out[v, rows, :] = term(v, g, r) + onat[v, rows, :] * fld[0, v, g, r]

    @functools.partial(over, lo, hi)
    def _(g):
        backward(steps - 1, g, True)

        @when(~is_last)
        def _():
            finish(g, lambda v, g, r: ret[v, g, r])
        if helping:
            @when(is_last)
            def _():
                give_back(g).start()

    @when(is_last)
    def _():
        @functools.partial(over, 0, groups)
        def _(g):
            finish(g, lambda v, g, r: wgt[0, v, g, r])

    if helping:
        @when(is_first)
        def _():
            @functools.partial(over, keep, groups)
            def _(g):
                give_back(g).wait_recv()
                finish(g, lambda v, g, r: ret[v, g, r])

    def sent(copies):
        for copy in copies:
            copy.wait_send()

    @functools.partial(over, lo, hi)
    def _(g):
        for n in range(steps + 1):
            sent(field_halo(n, g, k, 0))
        for i in range(steps):
            sent(flux_halo(back0 + i, g))
        onward(g).wait_send()

    @when(k > 0)
    def _():
        over(0, groups, lambda g: back(g).wait_send())

    @when(is_last)
    def _():
        over(0, groups, lambda g: sent(field_halo(edge, g, k, 0)))
        if helping:
            over(keep, groups, lambda g: give_back(g).wait_send())

    if helping:
        @when(is_first)
        def _():
            @functools.partial(over, keep, groups)
            def _(g):
                lend_state(g).wait_send()
                for n in range(steps):
                    lend_winds(n, g).wait_send()


def solution(mesh):
    windows, tiles = mesh.shape["win"], mesh.shape["tile"]

    def body(state, obs, trajectory, coupling, prec):
        block = state.shape[2:]
        variables, levels, cx, cy = block
        steps = trajectory.shape[2]
        groups = levels // GROUP
        keep = groups
        slots = 2 * steps + 2
        flat = (variables, levels * cx, cy)
        field = (variables, groups, cx, GROUP, cy)
        anywhere = pl.BlockSpec(memory_space=pltpu.HBM)
        f32 = jnp.float32
        result = pl.pallas_call(
            functools.partial(kernel, windows, tiles, keep),
            out_shape=jax.ShapeDtypeStruct(flat, f32),
            in_specs=[anywhere] * 5,
            out_specs=pl.BlockSpec(memory_space=pltpu.VMEM),
            scratch_shapes=[
                pltpu.VMEM(flat, f32),
                pltpu.VMEM(flat, f32),
                pltpu.VMEM((2 * steps, levels, cx, cy), trajectory.dtype),
                pltpu.SMEM(coupling.shape, f32),
                pltpu.SMEM(prec.shape, f32),
                pltpu.VMEM((steps + 2,) + field, f32),
                pltpu.VMEM((2 * steps, groups, cx, GROUP, cy), f32),
                pltpu.VMEM(field, f32),
                pltpu.VMEM((2,) + field, f32),
                pltpu.VMEM((steps,) + field, f32),
                pltpu.VMEM(field, f32),
                pltpu.VMEM((steps, 2, groups, variables, GROUP, cy), f32),
                pltpu.VMEM((slots, 2, groups, variables, GROUP, cy), f32),
                pltpu.VMEM((slots, groups, GROUP, cy), f32),
                pltpu.VMEM((slots, 2, groups, GROUP, cy), f32),
                pltpu.SemaphoreType.DMA((groups + steps + 3,)),
                pltpu.SemaphoreType.DMA((slots, 4, groups)),
                pltpu.SemaphoreType.DMA((slots, 4, groups)),
                pltpu.SemaphoreType.DMA((2, groups)),
                pltpu.SemaphoreType.DMA((2, groups)),
                pltpu.SemaphoreType.DMA((2 + steps, groups)),
                pltpu.SemaphoreType.DMA((2 + steps, groups)),
            ],
            compiler_params=pltpu.CompilerParams(
                collective_id=0, has_side_effects=True, vmem_limit_bytes=48 * 2**20),
        )(*[pltpu.with_memory_space_constraint(x, pltpu.HBM) for x in (
            state.reshape(flat), obs.reshape(flat),
            trajectory.reshape((2 * steps, levels, cx, cy)), coupling, prec)])
        return result.reshape((1, 1) + block)

    spec = P("win", "tile", None, None, None, None)
    return jax.shard_map(
        body, mesh=mesh,
        in_specs=(spec, spec, P("win", "tile", None, None, None, None, None), P(), P()),
        out_specs=spec, check_vma=False)
```

profile of v0, /device:TPU:1, one launch (start us, length us, event | category | flops | bytes accessed | tf_op | source)
XLA Modules:
  0.0 64.6 jit_solution(2240426790670831975)
XLA Ops:
  0.0 63.8 %shard_map.55 = f32[5,256,128]{2,1,0:T(8,128)S(1)} custom-call(f32[5,256,128]{2,1,0:T(8,128)} %bitcast.5, f32[5,256,128]{2,1,0:T(8,128)} %bitcast.6, bf16[6,32,8,128]{3,2,1,0:T(8,128)(2,1)} %bitcast.7, f32[5,5]{1,0:T(8,128)} %coupling.1, f32[5,32]{1,0:T(8,128)} %prec.1), custom_call_target="tpu_custom_call" | custom-call | tf_op jit(solution)/shard_map/pallas_call | solution.py:489
  63.8 0.8 %copy.7 = f32[1,1,5,32,8,128]{5,4,3,2,1,0:T(8,128)} copy(f32[1,1,5,32,8,128]{5,4,3,2,1,0:T(8,128)S(1)} %bitcast.4) | data formatting | bytes 1310720
where the time goes:
time: 64.8 us; the launch traced here: 64.6 us
  Pallas kernels  63.8 us (98%)
  local copies, waits for them, and re-layouts  0.84 us (1%)
    pallas_call x1, Pallas kernels, body(): pl.pallas_call(functools.partial(kernel, windows, tiles, keep), out_shape...  63.8 us

commit v1 on v0

--- a/solution.py
+++ b/solution.py
@@ -27,11 +27,12 @@
     before_x, after_x = lax.rem(t + tiles - TY, tiles), lax.rem(t + TY, tiles)
     before_y, after_y = lax.rem(t + tiles - 1, tiles), lax.rem(t + 1, tiles)
     around = (before_x, after_x, before_y, after_y)
-    is_first, is_last = k == 0, k == end
-    lo, hi = jnp.where(is_last, keep, 0), jnp.where(is_first, keep, groups)
+    lender = end - 2
+    is_first, is_last, lends = k == 0, k == end, k == lender
+    lo, hi = jnp.where(is_last, keep, 0), jnp.where(lends, keep, groups)
     sel = jnp.where(is_last, 1, 0)
-    nxt = jnp.where(is_last, 1, k + 1)
-    edges = jnp.where(is_last, edge, 0)
+    nxt = jnp.where(is_last, lender + 1, k + 1)
+    lone = jnp.where(is_last, 0, jnp.where(lends, keep, groups))
 
     def when(cond):
         return pl.when(cond)
@@ -67,7 +68,6 @@
         pl.semaphore_signal(barrier, inc=1, device_id={"win": win})
         for other in others:
             pl.semaphore_signal(barrier, inc=1, device_id={"win": win, "tile": other})
-        return
 
     for other in around:
         pl.semaphore_signal(barrier, inc=1, device_id={"tile": other})
@@ -82,19 +82,14 @@
 
     met = 4 + 5 * jnp.where(k < end, 1, 0) + 5 * jnp.where(k > 0, 1, 0)
     if helping:
-        @when(is_first)
+        @when(lends)
         def _():
             greet(end, ())
 
-        @when(k == 1)
-        def _():
-            greet(end, around)
-
         @when(is_last)
         def _():
-            greet(0, ())
-            greet(1, around)
-        met = met + jnp.where(is_first, 1, 0) + 5 * jnp.where(k == 1, 1, 0) + 6 * jnp.where(is_last, 1, 0)
+            greet(lender, ())
+        met = met + jnp.where(lends | is_last, 1, 0)
 
     shape = (GROUP, cy)
     lane = lax.broadcasted_iota(jnp.int32, shape, 1)
@@ -132,9 +127,9 @@
             send_sem=wsend.at[0, g], recv_sem=wrecv.at[0, g], device_id={"win": nxt})
 
     def back(g):
-        source = jnp.where(k == 1, jnp.where(g < keep, 0, end), k - 1)
+        source = jnp.where((k == lender + 1) & (g >= keep), end, k - 1)
         return pltpu.make_async_remote_copy(
-            src_ref=wgt.at[0, :, g], dst_ref=gf.at[0, :, g],
+            src_ref=wgt.at[:, g], dst_ref=gf.at[0, :, g],
             send_sem=wsend.at[1, g], recv_sem=wrecv.at[1, g], device_id={"win": source})
 
     def lend_state(g):
@@ -150,7 +145,7 @@
     def give_back(g):
         return pltpu.make_async_remote_copy(
             src_ref=ret.at[:, g], dst_ref=ret.at[:, g],
-            send_sem=msend.at[1, g], recv_sem=mrecv.at[1, g], device_id={"win": 0})
+            send_sem=msend.at[1, g], recv_sem=mrecv.at[1, g], device_id={"win": lender})
 
     def place(v, r):
         return v * cx + r
@@ -196,7 +191,7 @@
         if g == order[0]:
             pl.semaphore_wait(barrier, met)
         if g >= keep:
-            @when(is_first)
+            @when(lends)
             def _():
                 lend_state(g).start()
 
@@ -222,7 +217,7 @@
                 g = lax.rem(i + keep, groups)
                 convert_winds(n, g)
                 if helping:
-                    @when(is_first & (g >= keep))
+                    @when(lends & (g >= keep))
                     def _():
                         lend_winds(n, g).start()
             over(0, groups, one)
@@ -239,13 +234,10 @@
                 for copy in field_halo(0, g, k, 1):
                     copy.start()
 
-    @when(is_last)
-    def _():
-        @functools.partial(over, 0, groups)
-        def _(g):
-            pack_state(g, 0, edge)
-            for copy in field_halo(edge, g, k, 0):
-                copy.start()
+    def ship_edge(g):
+        pack_state(g, 0, edge)
+        for copy in field_halo(edge, g, k, 0):
+            copy.start()
 
     def forward(n, g):
         if helping:
@@ -287,11 +279,14 @@
 
     @functools.partial(over, 0, steps)
     def _(n):
+        @when(n == min(1, steps - 1))
+        def _():
+            over(lone, groups, ship_edge)
         over(lo, hi, lambda g: forward(n, g))
 
     prec_in.wait()
 
-    def stencil(g, row, rim, index):
+    def stencil(g, row, rim):
         scale = []
         for v in range(variables):
             s = jnp.zeros(shape, jnp.float32)
@@ -305,7 +300,7 @@
                 north, south = sides(here[v], rim, v, r)
                 smooth = (1.0 + 4.0 * smooth_weight) * here[v] - smooth_weight * (
                     east[v] + west[v] + north + south)
-                wgt[index, v, g, r] = scale[v] * smooth
+                wgt[v, g, r] = scale[v] * smooth
             west, here = here, east
 
     def start_window(g):
@@ -314,11 +309,13 @@
                 return [xr[0, 1, g, v] for v in range(variables)]
             if r == cx:
                 return [xr[0, 0, g, v] for v in range(variables)]
-            return [fld[sel, v, g, r] for v in range(variables)]
-        stencil(g, row, rims(yr[0, 0, g], yr[0, 1, g]), sel)
+            return [fld[0, v, g, r] for v in range(variables)]
+        stencil(g, row, rims(yr[0, 0, g], yr[0, 1, g]))
 
     def mismatch(g):
-        @when(is_last)
+        edges = jnp.where(g >= lone, edge, 0)
+
+        @when(g >= lone)
         def _():
             receive(edge, g)
         receive(moved, g)
@@ -330,16 +327,16 @@
             if r == cx:
                 return [xr[edges, 0, g, v] - xr[moved, 0, g, v] for v in range(variables)]
             return [fld[0, v, g, r] - arrived[v, g, r] for v in range(variables)]
-        stencil(g, row, rims(yr[edges, 0, g] - yr[moved, 0, g], yr[edges, 1, g] - yr[moved, 1, g]), 0)
+        stencil(g, row, rims(yr[edges, 0, g] - yr[moved, 0, g], yr[edges, 1, g] - yr[moved, 1, g]))
         back(g).start()
 
     @when(k > 0)
     def _():
         over(0, groups, mismatch)
 
-    @when(is_first | is_last)
-    def _():
-        over(lo, hi, start_window)
+    @when(is_first)
+    def _():
+        over(0, groups, start_window)
 
     def begin_back(g):
         back(g).wait_recv()
@@ -386,7 +383,7 @@
                 for b in range(variables):
                     total = total + cs[b, v] * values[b]
                 if final:
-                    ret[v, g, r] = wgt[sel, v, g, r] - total
+                    ret[v, g, r] = total
                     continue
                 gf[i + 1, v, g, r] = total
                 if r == 0:
@@ -408,11 +405,12 @@
 
     obs_in.wait()
 
-    def finish(g, term):
+    def finish(g, has_next):
         for v in range(variables):
             for r in range(cx):
                 rows = rows_of(g, r)
-                out[v, rows, :] = term(v, g, r) + onat[v, rows, :] * fld[0, v, g, r]
+                own = wgt[v, g, r] + onat[v, rows, :] * fld[0, v, g, r]
+                out[v, rows, :] = own - ret[v, g, r] if has_next else own
 
     @functools.partial(over, lo, hi)
     def _(g):
@@ -420,7 +418,7 @@
 
         @when(~is_last)
         def _():
-            finish(g, lambda v, g, r: ret[v, g, r])
+            finish(g, True)
         if helping:
             @when(is_last)
             def _():
@@ -430,15 +428,15 @@
     def _():
         @functools.partial(over, 0, groups)
         def _(g):
-            finish(g, lambda v, g, r: wgt[0, v, g, r])
+            finish(g, False)
 
     if helping:
-        @when(is_first)
+        @when(lends)
         def _():
             @functools.partial(over, keep, groups)
             def _(g):
                 give_back(g).wait_recv()
-                finish(g, lambda v, g, r: ret[v, g, r])
+                finish(g, True)
 
     def sent(copies):
         for copy in copies:
@@ -456,14 +454,14 @@
     def _():
         over(0, groups, lambda g: back(g).wait_send())
 
-    @when(is_last)
-    def _():
-        over(0, groups, lambda g: sent(field_halo(edge, g, k, 0)))
-        if helping:
+    over(lone, groups, lambda g: sent(field_halo(edge, g, k, 0)))
+    if helping:
+        @when(is_last)
+        def _():
             over(keep, groups, lambda g: give_back(g).wait_send())
 
     if helping:
-        @when(is_first)
+        @when(lends)
         def _():
             @functools.partial(over, keep, groups)
             def _(g):
@@ -480,7 +478,7 @@
         variables, levels, cx, cy = block
         steps = trajectory.shape[2]
         groups = levels // GROUP
-        keep = groups
+        keep = groups // 2 if windows > 3 else groups
         slots = 2 * steps + 2
         flat = (variables, levels * cx, cy)
         field = (variables, groups, cx, GROUP, cy)
@@ -500,7 +498,7 @@
                 pltpu.VMEM((steps + 2,) + field, f32),
                 pltpu.VMEM((2 * steps, groups, cx, GROUP, cy), f32),
                 pltpu.VMEM(field, f32),
-                pltpu.VMEM((2,) + field, f32),
+                pltpu.VMEM(field, f32),
                 pltpu.VMEM((steps,) + field, f32),
                 pltpu.VMEM(field, f32),
                 pltpu.VMEM((steps, 2, groups, variables, GROUP, cy), f32),

time: 64.8 us -> 58.6 us (0.904)
  the two profiles are of different devices: /device:TPU:1 before, /device:TPU:4 now
where the time goes in v1:
time: 58.6 us; the launch traced here: 58.5 us
  Pallas kernels  57.6 us (98%)
  local copies, waits for them, and re-layouts  0.84 us (1%)
    pallas_call x1, Pallas kernels, body(): pl.pallas_call(functools.partial(kernel, windows, tiles, keep), out_shape...  57.6 us

profile of v1, /device:TPU:4, one launch (start us, length us, event | category | flops | bytes accessed | tf_op | source)
XLA Modules:
  0.0 58.5 jit_solution(11268674423146187498)
XLA Ops:
  0.0 57.6 %shard_map.55 = f32[5,256,128]{2,1,0:T(8,128)S(1)} custom-call(f32[5,256,128]{2,1,0:T(8,128)} %bitcast.5, f32[5,256,128]{2,1,0:T(8,128)} %bitcast.6, bf16[6,32,8,128]{3,2,1,0:T(8,128)(2,1)} %bitcast.7, f32[5,5]{1,0:T(8,128)} %coupling.1, f32[5,32]{1,0:T(8,128)} %prec.1), custom_call_target="tpu_custom_call" | custom-call | tf_op jit(solution)/shard_map/pallas_call | solution.py:487
  57.7 0.8 %copy.7 = f32[1,1,5,32,8,128]{5,4,3,2,1,0:T(8,128)} copy(f32[1,1,5,32,8,128]{5,4,3,2,1,0:T(8,128)S(1)} %bitcast.4) | data formatting | bytes 1310720

commit v2 on v1

--- a/solution.py
+++ b/solution.py
@@ -13,14 +13,15 @@
 smooth_weight = 0.2
 
 
-def kernel(windows, tiles, keep, state, obs, winds, coupling, prec, out,
-           nat, onat, wnat, cs, ps, fld, wr, arrived, wgt, gf, ret, xs, xr, ys, yr,
-           load, hsend, hrecv, wsend, wrecv, msend, mrecv):
+def kernel(windows, tiles, keep, hold, state, obs, winds, coupling, prec, out,
+           nat, onat, wnat, cs, ps, fld, wr, arrived, wgt, gf, ret, xs, xr, ys, yr, xw, xe, ye,
+           load, hsend, hrecv, wsend, wrecv, msend, mrecv, esend, erecv):
     steps, groups, cx, cy = wr.shape[0] // 2, wr.shape[1], wr.shape[2], wr.shape[4]
     variables = fld.shape[1]
     span = GROUP * cx
     end = windows - 1
-    moved, edge, back0 = steps, steps + 1, steps + 2
+    gap, back0 = steps, steps + 1
+    breeze, early = back0 + steps, back0 + steps + 1
     helping = keep < groups
     k = lax.axis_index("win")
     t = lax.axis_index("tile")
@@ -30,9 +31,9 @@
     lender = end - 2
     is_first, is_last, lends = k == 0, k == end, k == lender
     lo, hi = jnp.where(is_last, keep, 0), jnp.where(lends, keep, groups)
+    back_lo, back_hi = jnp.where(is_last, hold, 0), jnp.where(lends, hold, groups)
     sel = jnp.where(is_last, 1, 0)
     nxt = jnp.where(is_last, lender + 1, k + 1)
-    lone = jnp.where(is_last, 0, jnp.where(lends, keep, groups))
 
     def when(cond):
         return pl.when(cond)
@@ -97,7 +98,8 @@
     pair, odd = lane // 2, lane % 2 == 1
     at_start, at_end = lane == 0, lane == cy - 1
 
-    def halo(slot, g, win, low, high):
+    def halo(slot, g, win, low, high, into=None):
+        into = xr.at[slot] if into is None else into
         made = []
         for side, to in enumerate((before_y, after_y)):
             made.append(pltpu.make_async_remote_copy(
@@ -106,20 +108,43 @@
                 device_id={"win": win, "tile": to}))
         for side, (to, rows) in enumerate(((before_x, low), (after_x, high))):
             made.append(pltpu.make_async_remote_copy(
-                src_ref=rows, dst_ref=xr.at[slot, side, g],
+                src_ref=rows, dst_ref=into.at[side, g],
                 send_sem=hsend.at[slot, 2 + side, g], recv_sem=hrecv.at[slot, 2 + side, g],
                 device_id={"win": win, "tile": to}))
         return made
 
-    def field_halo(slot, g, win, index):
-        return halo(slot, g, win, fld.at[index, :, g, 0], fld.at[index, :, g, cx - 1])
-
-    def flux_halo(slot, g):
-        return halo(slot, g, k, xs.at[slot - back0, 0, g], xs.at[slot - back0, 1, g])
+    def field_halo(slot, g, index):
+        return halo(slot, g, k, fld.at[index, :, g, 0], fld.at[index, :, g, cx - 1])
+
+    def gap_halo(g):
+        return halo(gap, g, nxt, xs.at[0, 0, g], xs.at[0, 1, g])
+
+    def weighted_halo(g):
+        return halo(back0, g, source(g, hold), wgt.at[:, g, 0], wgt.at[:, g, cx - 1])
+
+    def flux_halo(i, g):
+        return halo(back0 + i, g, k, xs.at[i, 0, g], xs.at[i, 1, g])
+
+    def breeze_halo(g):
+        u = wr.at[2 * steps - 2, g]
+        return halo(breeze, g, k, u.at[0], u.at[cx - 1], xw)
 
     def receive(slot, g):
         for copy in halo(slot, g, k, xr.at[slot, 0, g], xr.at[slot, 1, g]):
             copy.wait_recv()
+
+    def source(g, bound):
+        return jnp.where((k == lender + 1) & (g >= bound), end, k - 1)
+
+    def early_edges(g):
+        made = []
+        for i, (src, dst) in enumerate((
+            (fld.at[0, :, g, 0], xe.at[0, g]), (fld.at[0, :, g, cx - 1], xe.at[1, g]), (ys.at[early, g], ye.at[g]),
+        )):
+            made.append(pltpu.make_async_remote_copy(
+                src_ref=src, dst_ref=dst, send_sem=esend.at[i, g], recv_sem=erecv.at[i, g],
+                device_id={"win": source(g, keep)}))
+        return made
 
     def onward(g):
         return pltpu.make_async_remote_copy(
@@ -127,10 +152,9 @@
             send_sem=wsend.at[0, g], recv_sem=wrecv.at[0, g], device_id={"win": nxt})
 
     def back(g):
-        source = jnp.where((k == lender + 1) & (g >= keep), end, k - 1)
         return pltpu.make_async_remote_copy(
             src_ref=wgt.at[:, g], dst_ref=gf.at[0, :, g],
-            send_sem=wsend.at[1, g], recv_sem=wrecv.at[1, g], device_id={"win": source})
+            send_sem=wsend.at[1, g], recv_sem=wrecv.at[1, g], device_id={"win": source(g, hold)})
 
     def lend_state(g):
         return pltpu.make_async_remote_copy(
@@ -175,12 +199,16 @@
             for r in range(cx):
                 fld[0, v, g, r] = nat[v, rows_of(g, r), :]
 
-    def pack_state(g, index, slot):
+    def pack_state(g, index):
         packed = jnp.zeros(shape, jnp.float32)
         for v in range(variables):
             for r in range(cx):
                 packed = pack(packed, fld[index, v, g, r], v, r)
-        ys[slot, g] = packed
+        return packed
+
+    def start(copies):
+        for copy in copies:
+            copy.start()
 
     def over(a, b, f):
         lax.fori_loop(a, b, lambda g, c: (f(g), c)[1], 0)
@@ -195,11 +223,17 @@
             def _():
                 lend_state(g).start()
 
+        packed = pack_state(g, 0)
+        ys[0, g] = packed
+        ys[early, g] = packed
+
         @when((k < end) & (g < hi))
         def _():
-            pack_state(g, 0, 0)
-            for copy in field_halo(0, g, k, 0):
-                copy.start()
+            start(field_halo(0, g, 0))
+
+    @when(k > 0)
+    def _():
+        over(0, groups, lambda g: start(early_edges(g)))
 
     def convert_winds(n, g):
         for way in range(2):
@@ -230,30 +264,39 @@
             @functools.partial(over, keep, groups)
             def _(g):
                 lend_state(g).wait_recv()
-                pack_state(g, 1, 0)
-                for copy in field_halo(0, g, k, 1):
-                    copy.start()
-
-    def ship_edge(g):
-        pack_state(g, 0, edge)
-        for copy in field_halo(edge, g, k, 0):
-            copy.start()
-
-    def forward(n, g):
-        if helping:
-            @when(is_last)
-            def _():
-                lend_winds(n, g).wait_recv()
+                ys[0, g] = pack_state(g, 1)
+                start(field_halo(0, g, 1))
+
+    def ship_breeze(g):
+        n = steps - 1
+        packed = jnp.zeros(shape, jnp.float32)
+        for r in range(cx):
+            packed = pack(packed, wr[2 * n + 1, g, r], 0, r)
+        total = packed
+        for v in range(1, variables):
+            total = total + pltpu.roll(packed, 2 * place(v, 0), 1)
+        ys[breeze, g] = total
+        start(breeze_halo(g))
+
+    def forward(n, g, final):
+        if not final:
+            if helping:
+                @when(is_last)
+                def _():
+                    lend_winds(n, g).wait_recv()
         receive(n, g)
-        source = jnp.where(n == 0, sel, n + 1)
+        index = jnp.where(n == 0, sel, n + 1)
         rim = rims(yr[n, 0, g], yr[n, 1, g])
+        if final:
+            for copy in early_edges(g):
+                copy.wait_recv()
 
         def row(r):
             if r < 0:
                 return [xr[n, 1, g, v] for v in range(variables)]
             if r == cx:
                 return [xr[n, 0, g, v] for v in range(variables)]
-            return [fld[source, v, g, r] for v in range(variables)]
+            return [fld[index, v, g, r] for v in range(variables)]
 
         west, here = row(-1), row(0)
         packed = jnp.zeros(shape, jnp.float32)
@@ -266,27 +309,41 @@
                 for b in range(variables):
                     total = total + cs[v, b] * here[b]
                 fld[n + 2, v, g, r] = total
+                if final and r == 0:
+                    xs[0, 0, g, v] = xe[0, g, v] - total
+                if final and r == cx - 1:
+                    xs[0, 1, g, v] = xe[1, g, v] - total
                 packed = pack(packed, total, v, r)
             west, here = here, east
-        ys[n + 1, g] = packed
-        ends = n == steps - 1
-        for copy in field_halo(n + 1, g, jnp.where(ends, nxt, k), n + 2):
-            copy.start()
-
-        @when(ends)
-        def _():
+        if final:
+            ys[gap, g] = ye[g] - packed
+            start(gap_halo(g))
             onward(g).start()
-
-    @functools.partial(over, 0, steps)
+        else:
+            ys[n + 1, g] = packed
+            start(field_halo(n + 1, g, n + 2))
+
+    def ship_breezes():
+        if helping:
+            @when(is_last)
+            def _():
+                over(keep, groups, lambda g: lend_winds(steps - 1, g).wait_recv())
+        over(back_lo, back_hi, ship_breeze)
+
+    @functools.partial(over, 0, steps - 1)
     def _(n):
-        @when(n == min(1, steps - 1))
-        def _():
-            over(lone, groups, ship_edge)
-        over(lo, hi, lambda g: forward(n, g))
+        @when(n == min(1, steps - 2))
+        def _():
+            ship_breezes()
+        over(lo, hi, lambda g: forward(n, g, False))
+
+    if steps < 2:
+        ship_breezes()
+    over(lo, hi, lambda g: forward(steps - 1, g, True))
 
     prec_in.wait()
 
-    def stencil(g, row, rim):
+    def stencil(g, row, rim, keeps):
         scale = []
         for v in range(variables):
             s = jnp.zeros(shape, jnp.float32)
@@ -294,14 +351,19 @@
                 s = jnp.where(level == j, ps[v, g * GROUP + j], s)
             scale.append(s)
         west, here = row(-1), row(0)
+        packed = jnp.zeros(shape, jnp.float32)
         for r in range(cx):
             east = row(r + 1)
             for v in range(variables):
                 north, south = sides(here[v], rim, v, r)
                 smooth = (1.0 + 4.0 * smooth_weight) * here[v] - smooth_weight * (
                     east[v] + west[v] + north + south)
-                wgt[v, g, r] = scale[v] * smooth
+                total = scale[v] * smooth
+                wgt[v, g, r] = total
+                if keeps:
+                    packed = pack(packed, total, v, r)
             west, here = here, east
+        return packed
 
     def start_window(g):
         def row(r):
@@ -310,24 +372,20 @@
             if r == cx:
                 return [xr[0, 0, g, v] for v in range(variables)]
             return [fld[0, v, g, r] for v in range(variables)]
-        stencil(g, row, rims(yr[0, 0, g], yr[0, 1, g]))
+        stencil(g, row, rims(yr[0, 0, g], yr[0, 1, g]), False)
 
     def mismatch(g):
-        edges = jnp.where(g >= lone, edge, 0)
-
-        @when(g >= lone)
-        def _():
-            receive(edge, g)
-        receive(moved, g)
+        receive(gap, g)
         onward(g).wait_recv()
 
         def row(r):
             if r < 0:
-                return [xr[edges, 1, g, v] - xr[moved, 1, g, v] for v in range(variables)]
+                return [xr[gap, 1, g, v] for v in range(variables)]
             if r == cx:
-                return [xr[edges, 0, g, v] - xr[moved, 0, g, v] for v in range(variables)]
+                return [xr[gap, 0, g, v] for v in range(variables)]
             return [fld[0, v, g, r] - arrived[v, g, r] for v in range(variables)]
-        stencil(g, row, rims(yr[edges, 0, g] - yr[moved, 0, g], yr[edges, 1, g] - yr[moved, 1, g]))
+        ys[back0, g] = stencil(g, row, rims(yr[gap, 0, g], yr[gap, 1, g]), True)
+        start(weighted_halo(g))
         back(g).start()
 
     @when(k > 0)
@@ -338,34 +396,29 @@
     def _():
         over(0, groups, start_window)
 
-    def begin_back(g):
-        back(g).wait_recv()
-        n = steps - 1
-        packed = jnp.zeros(shape, jnp.float32)
-        for r in range(cx):
-            u, w = wr[2 * n, g, r], wr[2 * n + 1, g, r]
-            for v in range(variables):
-                value = gf[0, v, g, r]
-                if r == 0:
-                    xs[0, 0, g, v] = u * value
-                if r == cx - 1:
-                    xs[0, 1, g, v] = u * value
-                packed = pack(packed, w * value, v, r)
-        ys[back0, g] = packed
-        for copy in flux_halo(back0, g):
-            copy.start()
-
-    def backward(i, g, final):
+    def backward(i, g):
         n = steps - 1 - i
         slot = back0 + i
+        first, final = i == 0, i == steps - 1
+        if first:
+            for copy in breeze_halo(g):
+                copy.wait_recv()
+            back(g).wait_recv()
         receive(slot, g)
-        rim = rims(yr[slot, 0, g], yr[slot, 1, g])
+        rim = [yr[slot, side, g] for side in range(2)]
+        if first:
+            rim = [rim[side] * yr[breeze, side, g] for side in range(2)]
+        rim = rims(*rim)
+
+        def beyond(side):
+            values = [xr[slot, side, g, v] for v in range(variables)]
+            return [value * xw[side, g] for value in values] if first else values
 
         def row(r):
             if r < 0:
-                return None, [xr[slot, 1, g, v] for v in range(variables)]
+                return None, beyond(1)
             if r == cx:
-                return None, [xr[slot, 0, g, v] for v in range(variables)]
+                return None, beyond(0)
             u = wr[2 * n, g, r]
             values = [gf[i, v, g, r] for v in range(variables)]
             return values, [u * value for value in values]
@@ -394,14 +447,10 @@
             west, values, here = here, values_east, east
         if not final:
             ys[slot + 1, g] = packed
-            for copy in flux_halo(slot + 1, g):
-                copy.start()
-
-    over(lo, hi, begin_back)
-
-    @functools.partial(over, 0, steps - 1)
-    def _(i):
-        over(lo, hi, lambda g: backward(i, g, False))
+            start(flux_halo(i + 1, g))
+
+    for i in range(steps - 1):
+        over(back_lo, back_hi, functools.partial(backward, i))
 
     obs_in.wait()
 
@@ -412,9 +461,9 @@
                 own = wgt[v, g, r] + onat[v, rows, :] * fld[0, v, g, r]
                 out[v, rows, :] = own - ret[v, g, r] if has_next else own
 
-    @functools.partial(over, lo, hi)
+    @functools.partial(over, back_lo, back_hi)
     def _(g):
-        backward(steps - 1, g, True)
+        backward(steps - 1, g)
 
         @when(~is_last)
         def _():
@@ -433,7 +482,7 @@
     if helping:
         @when(lends)
         def _():
-            @functools.partial(over, keep, groups)
+            @functools.partial(over, hold, groups)
             def _(g):
                 give_back(g).wait_recv()
                 finish(g, True)
@@ -444,21 +493,29 @@
 
     @functools.partial(over, lo, hi)
     def _(g):
-        for n in range(steps + 1):
-            sent(field_halo(n, g, k, 0))
-        for i in range(steps):
-            sent(flux_halo(back0 + i, g))
+        for n in range(steps):
+            sent(field_halo(n, g, 0))
+        sent(gap_halo(g))
         onward(g).wait_send()
 
+    @functools.partial(over, back_lo, back_hi)
+    def _(g):
+        for i in range(1, steps):
+            sent(flux_halo(i, g))
+        sent(breeze_halo(g))
+
     @when(k > 0)
     def _():
-        over(0, groups, lambda g: back(g).wait_send())
-
-    over(lone, groups, lambda g: sent(field_halo(edge, g, k, 0)))
+        @functools.partial(over, 0, groups)
+        def _(g):
+            sent(weighted_halo(g))
+            sent(early_edges(g))
+            back(g).wait_send()
+
     if helping:
         @when(is_last)
         def _():
-            over(keep, groups, lambda g: give_back(g).wait_send())
+            over(hold, groups, lambda g: give_back(g).wait_send())
 
     if helping:
         @when(lends)
@@ -478,14 +535,14 @@
         variables, levels, cx, cy = block
         steps = trajectory.shape[2]
         groups = levels // GROUP
-        keep = groups // 2 if windows > 3 else groups
-        slots = 2 * steps + 2
+        keep, hold = (groups // 2, groups - groups // 4) if windows > 3 else (groups, groups)
+        slots = 2 * steps + 3
         flat = (variables, levels * cx, cy)
         field = (variables, groups, cx, GROUP, cy)
         anywhere = pl.BlockSpec(memory_space=pltpu.HBM)
         f32 = jnp.float32
         result = pl.pallas_call(
-            functools.partial(kernel, windows, tiles, keep),
+            functools.partial(kernel, windows, tiles, keep, hold),
             out_shape=jax.ShapeDtypeStruct(flat, f32),
             in_specs=[anywhere] * 5,
             out_specs=pl.BlockSpec(memory_space=pltpu.VMEM),
@@ -505,6 +562,9 @@
                 pltpu.VMEM((slots, 2, groups, variables, GROUP, cy), f32),
                 pltpu.VMEM((slots, groups, GROUP, cy), f32),
                 pltpu.VMEM((slots, 2, groups, GROUP, cy), f32),
+                pltpu.VMEM((2, groups, GROUP, cy), f32),
+                pltpu.VMEM((2, groups, variables, GROUP, cy), f32),
+                pltpu.VMEM((groups, GROUP, cy), f32),
                 pltpu.SemaphoreType.DMA((groups + steps + 3,)),
                 pltpu.SemaphoreType.DMA((slots, 4, groups)),
                 pltpu.SemaphoreType.DMA((slots, 4, groups)),
@@ -512,6 +572,8 @@
                 pltpu.SemaphoreType.DMA((2, groups)),
                 pltpu.SemaphoreType.DMA((2 + steps, groups)),
                 pltpu.SemaphoreType.DMA((2 + steps, groups)),
+                pltpu.SemaphoreType.DMA((3, groups)),
+                pltpu.SemaphoreType.DMA((3, groups)),
             ],
             compiler_params=pltpu.CompilerParams(
                 collective_id=0, has_side_effects=True, vmem_limit_bytes=48 * 2**20),

time: 58.6 us -> 54.6 us (0.932)
  the two profiles are of different devices: /device:TPU:4 before, /device:TPU:1 now
where the time goes in v2:
time: 54.6 us; the launch traced here: 54.4 us
  Pallas kernels  53.6 us (98%)
  local copies, waits for them, and re-layouts  0.84 us (2%)
    pallas_call x1, Pallas kernels, body(): pl.pallas_call(functools.partial(kernel, windows, tiles, keep, hold), out...  53.6 us

profile of v2, /device:TPU:1, one launch (start us, length us, event | category | flops | bytes accessed | tf_op | source)
XLA Modules:
  0.0 54.4 jit_solution(13091419861199421701)
XLA Ops:
  0.0 53.6 %shard_map.55 = f32[5,256,128]{2,1,0:T(8,128)S(1)} custom-call(f32[5,256,128]{2,1,0:T(8,128)} %bitcast.5, f32[5,256,128]{2,1,0:T(8,128)} %bitcast.6, bf16[6,32,8,128]{3,2,1,0:T(8,128)(2,1)} %bitcast.7, f32[5,5]{1,0:T(8,128)} %coupling.1, f32[5,32]{1,0:T(8,128)} %prec.1), custom_call_target="tpu_custom_call" | custom-call | tf_op jit(solution)/shard_map/pallas_call | solution.py:544
  53.6 0.8 %copy.7 = f32[1,1,5,32,8,128]{5,4,3,2,1,0:T(8,128)} copy(f32[1,1,5,32,8,128]{5,4,3,2,1,0:T(8,128)S(1)} %bitcast.4) | data formatting | bytes 1310720

commit v3 on v2

--- a/solution.py
+++ b/solution.py
@@ -14,14 +14,14 @@
 
 
 def kernel(windows, tiles, keep, hold, state, obs, winds, coupling, prec, out,
-           nat, onat, wnat, cs, ps, fld, wr, arrived, wgt, gf, ret, xs, xr, ys, yr, xw, xe, ye,
-           load, hsend, hrecv, wsend, wrecv, msend, mrecv, esend, erecv):
+           nat, onat, wnat, cs, ps, fld, wr, arrived, wgt, gf, ret, xs, xr, ys, yr, yp, xe, ye, xw, yw,
+           load, hsend, hrecv, wsend, wrecv, msend, mrecv, esend, erecv, fsend, frecv):
     steps, groups, cx, cy = wr.shape[0] // 2, wr.shape[1], wr.shape[2], wr.shape[4]
     variables = fld.shape[1]
     span = GROUP * cx
     end = windows - 1
     gap, back0 = steps, steps + 1
-    breeze, early = back0 + steps, back0 + steps + 1
+    half = GROUP // 2
     helping = keep < groups
     k = lax.axis_index("win")
     t = lax.axis_index("tile")
@@ -65,31 +65,29 @@
 
     barrier = pltpu.get_barrier_semaphore()
 
-    def greet(win, others):
+    def greet(win):
         pl.semaphore_signal(barrier, inc=1, device_id={"win": win})
-        for other in others:
-            pl.semaphore_signal(barrier, inc=1, device_id={"win": win, "tile": other})
 
     for other in around:
         pl.semaphore_signal(barrier, inc=1, device_id={"tile": other})
 
     @when(k < end)
     def _():
-        greet(k + 1, around)
+        greet(k + 1)
 
     @when(k > 0)
     def _():
-        greet(k - 1, around)
-
-    met = 4 + 5 * jnp.where(k < end, 1, 0) + 5 * jnp.where(k > 0, 1, 0)
+        greet(k - 1)
+
+    met = len(around) + jnp.where(k < end, 1, 0) + jnp.where(k > 0, 1, 0)
     if helping:
         @when(lends)
         def _():
-            greet(end, ())
+            greet(end)
 
         @when(is_last)
         def _():
-            greet(lender, ())
+            greet(lender)
         met = met + jnp.where(lends | is_last, 1, 0)
 
     shape = (GROUP, cy)
@@ -98,17 +96,16 @@
     pair, odd = lane // 2, lane % 2 == 1
     at_start, at_end = lane == 0, lane == cy - 1
 
-    def halo(slot, g, win, low, high, into=None):
-        into = xr.at[slot] if into is None else into
+    def halo(slot, g, win, low, high):
         made = []
         for side, to in enumerate((before_y, after_y)):
             made.append(pltpu.make_async_remote_copy(
-                src_ref=ys.at[slot, g], dst_ref=yr.at[slot, side, g],
+                src_ref=ys.at[slot, side, g], dst_ref=yr.at[slot, side, g],
                 send_sem=hsend.at[slot, side, g], recv_sem=hrecv.at[slot, side, g],
                 device_id={"win": win, "tile": to}))
         for side, (to, rows) in enumerate(((before_x, low), (after_x, high))):
             made.append(pltpu.make_async_remote_copy(
-                src_ref=rows, dst_ref=into.at[side, g],
+                src_ref=rows, dst_ref=xr.at[slot, side, g],
                 send_sem=hsend.at[slot, 2 + side, g], recv_sem=hrecv.at[slot, 2 + side, g],
                 device_id={"win": win, "tile": to}))
         return made
@@ -120,14 +117,10 @@
         return halo(gap, g, nxt, xs.at[0, 0, g], xs.at[0, 1, g])
 
     def weighted_halo(g):
-        return halo(back0, g, source(g, hold), wgt.at[:, g, 0], wgt.at[:, g, cx - 1])
+        return halo(back0, g, source(g, hold), xs.at[steps, 0, g], xs.at[steps, 1, g])
 
     def flux_halo(i, g):
         return halo(back0 + i, g, k, xs.at[i, 0, g], xs.at[i, 1, g])
-
-    def breeze_halo(g):
-        u = wr.at[2 * steps - 2, g]
-        return halo(breeze, g, k, u.at[0], u.at[cx - 1], xw)
 
     def receive(slot, g):
         for copy in halo(slot, g, k, xr.at[slot, 0, g], xr.at[slot, 1, g]):
@@ -136,15 +129,21 @@
     def source(g, bound):
         return jnp.where((k == lender + 1) & (g >= bound), end, k - 1)
 
-    def early_edges(g):
-        made = []
-        for i, (src, dst) in enumerate((
-            (fld.at[0, :, g, 0], xe.at[0, g]), (fld.at[0, :, g, cx - 1], xe.at[1, g]), (ys.at[early, g], ye.at[g]),
-        )):
-            made.append(pltpu.make_async_remote_copy(
-                src_ref=src, dst_ref=dst, send_sem=esend.at[i, g], recv_sem=erecv.at[i, g],
-                device_id={"win": source(g, keep)}))
-        return made
+    def local_edges(pieces, sends, arrives, g, win):
+        return [pltpu.make_async_remote_copy(
+            src_ref=src, dst_ref=dst, send_sem=sends.at[i, g], recv_sem=arrives.at[i, g], device_id={"win": win})
+            for i, (src, dst) in enumerate(pieces)]
+
+    def state_edges(g):
+        return local_edges((
+            (fld.at[0, :, g, 0], xe.at[0, g]), (fld.at[0, :, g, cx - 1], xe.at[1, g]), (yp.at[0, g], ye.at[g]),
+        ), esend, erecv, g, source(g, keep))
+
+    def wind_edges(g):
+        n = 2 * steps - 2
+        return local_edges((
+            (wr.at[n, g, 0], xw.at[0, g]), (wr.at[n, g, cx - 1], xw.at[1, g]), (yp.at[1, g], yw.at[g]),
+        ), fsend, frecv, g, k + 1)
 
     def onward(g):
         return pltpu.make_async_remote_copy(
@@ -178,8 +177,16 @@
         p = place(v, r)
         return jnp.where(pair == p, pltpu.roll(value, 2 * p + 1, 1), packed)
 
-    def rims(north, south):
-        return jnp.where(odd, north, pltpu.roll(south, 2, 1))
+    def fold(slot, g, packed):
+        upper = pltpu.roll(pltpu.roll(packed, half, 0), 1, 1)
+        ys[slot, 0, g] = jnp.where(odd, packed, upper)[:half]
+        ys[slot, 1, g] = jnp.where(odd, upper, packed)[:half]
+
+    def unfold(slot, g):
+        north, south = [jnp.concatenate([yr[slot, side, g]] * 2, axis=0) for side in range(2)]
+        north = jnp.where(level < half, north, pltpu.roll(north, cy - 1, 1))
+        south = jnp.where(level < half, pltpu.roll(south, 2, 1), pltpu.roll(south, 1, 1))
+        return jnp.where(odd, north, south)
 
     def sides(value, rim, v, r):
         edge_pair = pltpu.roll(rim, cy - 2 - 2 * place(v, r), 1)
@@ -224,8 +231,8 @@
                 lend_state(g).start()
 
         packed = pack_state(g, 0)
-        ys[0, g] = packed
-        ys[early, g] = packed
+        fold(0, g, packed)
+        yp[0, g] = packed
 
         @when((k < end) & (g < hi))
         def _():
@@ -233,7 +240,7 @@
 
     @when(k > 0)
     def _():
-        over(0, groups, lambda g: start(early_edges(g)))
+        over(0, groups, lambda g: start(state_edges(g)))
 
     def convert_winds(n, g):
         for way in range(2):
@@ -256,6 +263,17 @@
                         lend_winds(n, g).start()
             over(0, groups, one)
 
+        @functools.partial(over, 0, groups)
+        def _(g):
+            packed = jnp.zeros(shape, jnp.float32)
+            for r in range(cx):
+                packed = pack(packed, wr[2 * steps - 1, g, r], 0, r)
+            total = packed
+            for v in range(1, variables):
+                total = total + pltpu.roll(packed, 2 * place(v, 0), 1)
+            yp[1, g] = total
+            start(wind_edges(g))
+
     coupling_in.wait()
 
     if helping:
@@ -264,31 +282,19 @@
             @functools.partial(over, keep, groups)
             def _(g):
                 lend_state(g).wait_recv()
-                ys[0, g] = pack_state(g, 1)
+                fold(0, g, pack_state(g, 1))
                 start(field_halo(0, g, 1))
 
-    def ship_breeze(g):
-        n = steps - 1
-        packed = jnp.zeros(shape, jnp.float32)
-        for r in range(cx):
-            packed = pack(packed, wr[2 * n + 1, g, r], 0, r)
-        total = packed
-        for v in range(1, variables):
-            total = total + pltpu.roll(packed, 2 * place(v, 0), 1)
-        ys[breeze, g] = total
-        start(breeze_halo(g))
-
     def forward(n, g, final):
-        if not final:
-            if helping:
-                @when(is_last)
-                def _():
-                    lend_winds(n, g).wait_recv()
+        if helping:
+            @when(is_last)
+            def _():
+                lend_winds(n, g).wait_recv()
         receive(n, g)
         index = jnp.where(n == 0, sel, n + 1)
-        rim = rims(yr[n, 0, g], yr[n, 1, g])
+        rim = unfold(n, g)
         if final:
-            for copy in early_edges(g):
+            for copy in state_edges(g):
                 copy.wait_recv()
 
         def row(r):
@@ -316,29 +322,17 @@
                 packed = pack(packed, total, v, r)
             west, here = here, east
         if final:
-            ys[gap, g] = ye[g] - packed
+            fold(gap, g, ye[g] - packed)
             start(gap_halo(g))
             onward(g).start()
         else:
-            ys[n + 1, g] = packed
+            fold(n + 1, g, packed)
             start(field_halo(n + 1, g, n + 2))
-
-    def ship_breezes():
-        if helping:
-            @when(is_last)
-            def _():
-                over(keep, groups, lambda g: lend_winds(steps - 1, g).wait_recv())
-        over(back_lo, back_hi, ship_breeze)
 
     @functools.partial(over, 0, steps - 1)
     def _(n):
-        @when(n == min(1, steps - 2))
-        def _():
-            ship_breezes()
         over(lo, hi, lambda g: forward(n, g, False))
 
-    if steps < 2:
-        ship_breezes()
     over(lo, hi, lambda g: forward(steps - 1, g, True))
 
     prec_in.wait()
@@ -362,6 +356,10 @@
                 wgt[v, g, r] = total
                 if keeps:
                     packed = pack(packed, total, v, r)
+                if keeps and r == 0:
+                    xs[steps, 0, g, v] = xw[0, g] * total
+                if keeps and r == cx - 1:
+                    xs[steps, 1, g, v] = xw[1, g] * total
             west, here = here, east
         return packed
 
@@ -372,11 +370,13 @@
             if r == cx:
                 return [xr[0, 0, g, v] for v in range(variables)]
             return [fld[0, v, g, r] for v in range(variables)]
-        stencil(g, row, rims(yr[0, 0, g], yr[0, 1, g]), False)
+        stencil(g, row, unfold(0, g), False)
 
     def mismatch(g):
         receive(gap, g)
         onward(g).wait_recv()
+        for copy in wind_edges(g):
+            copy.wait_recv()
 
         def row(r):
             if r < 0:
@@ -384,7 +384,7 @@
             if r == cx:
                 return [xr[gap, 0, g, v] for v in range(variables)]
             return [fld[0, v, g, r] - arrived[v, g, r] for v in range(variables)]
-        ys[back0, g] = stencil(g, row, rims(yr[gap, 0, g], yr[gap, 1, g]), True)
+        fold(back0, g, yw[g] * stencil(g, row, unfold(gap, g), True))
         start(weighted_halo(g))
         back(g).start()
 
@@ -401,24 +401,15 @@
         slot = back0 + i
         first, final = i == 0, i == steps - 1
         if first:
-            for copy in breeze_halo(g):
-                copy.wait_recv()
             back(g).wait_recv()
         receive(slot, g)
-        rim = [yr[slot, side, g] for side in range(2)]
-        if first:
-            rim = [rim[side] * yr[breeze, side, g] for side in range(2)]
-        rim = rims(*rim)
-
-        def beyond(side):
-            values = [xr[slot, side, g, v] for v in range(variables)]
-            return [value * xw[side, g] for value in values] if first else values
+        rim = unfold(slot, g)
 
         def row(r):
             if r < 0:
-                return None, beyond(1)
+                return None, [xr[slot, 1, g, v] for v in range(variables)]
             if r == cx:
-                return None, beyond(0)
+                return None, [xr[slot, 0, g, v] for v in range(variables)]
             u = wr[2 * n, g, r]
             values = [gf[i, v, g, r] for v in range(variables)]
             return values, [u * value for value in values]
@@ -446,7 +437,7 @@
                 packed = pack(packed, w_next * total, v, r)
             west, values, here = here, values_east, east
         if not final:
-            ys[slot + 1, g] = packed
+            fold(slot + 1, g, packed)
             start(flux_halo(i + 1, g))
 
     for i in range(steps - 1):
@@ -502,15 +493,18 @@
     def _(g):
         for i in range(1, steps):
             sent(flux_halo(i, g))
-        sent(breeze_halo(g))
 
     @when(k > 0)
     def _():
         @functools.partial(over, 0, groups)
         def _(g):
             sent(weighted_halo(g))
-            sent(early_edges(g))
+            sent(state_edges(g))
             back(g).wait_send()
+
+    @when(k < end)
+    def _():
+        over(0, groups, lambda g: sent(wind_edges(g)))
 
     if helping:
         @when(is_last)
@@ -536,7 +530,7 @@
         steps = trajectory.shape[2]
         groups = levels // GROUP
         keep, hold = (groups // 2, groups - groups // 4) if windows > 3 else (groups, groups)
-        slots = 2 * steps + 3
+        slots, half = 2 * steps + 1, GROUP // 2
         flat = (variables, levels * cx, cy)
         field = (variables, groups, cx, GROUP, cy)
         anywhere = pl.BlockSpec(memory_space=pltpu.HBM)
@@ -558,12 +552,14 @@
                 pltpu.VMEM(field, f32),
                 pltpu.VMEM((steps,) + field, f32),
                 pltpu.VMEM(field, f32),
-                pltpu.VMEM((steps, 2, groups, variables, GROUP, cy), f32),
+                pltpu.VMEM((steps + 1, 2, groups, variables, GROUP, cy), f32),
                 pltpu.VMEM((slots, 2, groups, variables, GROUP, cy), f32),
-                pltpu.VMEM((slots, groups, GROUP, cy), f32),
-                pltpu.VMEM((slots, 2, groups, GROUP, cy), f32),
+                pltpu.VMEM((slots, 2, groups, half, cy), f32),
+                pltpu.VMEM((slots, 2, groups, half, cy), f32),
                 pltpu.VMEM((2, groups, GROUP, cy), f32),
                 pltpu.VMEM((2, groups, variables, GROUP, cy), f32),
+                pltpu.VMEM((groups, GROUP, cy), f32),
+                pltpu.VMEM((2, groups, GROUP, cy), f32),
                 pltpu.VMEM((groups, GROUP, cy), f32),
                 pltpu.SemaphoreType.DMA((groups + steps + 3,)),
                 pltpu.SemaphoreType.DMA((slots, 4, groups)),
@@ -574,6 +570,8 @@
                 pltpu.SemaphoreType.DMA((2 + steps, groups)),
                 pltpu.SemaphoreType.DMA((3, groups)),
                 pltpu.SemaphoreType.DMA((3, groups)),
+                pltpu.SemaphoreType.DMA((3, groups)),
+                pltpu.SemaphoreType.DMA((3, groups)),
             ],
             compiler_params=pltpu.CompilerParams(
                 collective_id=0, has_side_effects=True, vmem_limit_bytes=48 * 2**20),

time: 54.6 us -> 53.9 us (0.987)
  Pallas kernels: 53.6 us -> 52.8 us
    pallas_call x1, Pallas kernels: 53.6 us -> 52.8 us  [body(): pl.pallas_call(functools.partial(kernel, windows, tiles, keep, hold), out...]
where the time goes in v3:
time: 53.9 us; the launch traced here: 53.7 us
  Pallas kernels  52.8 us (98%)
  local copies, waits for them, and re-layouts  0.84 us (2%)
    pallas_call x1, Pallas kernels, body(): pl.pallas_call(functools.partial(kernel, windows, tiles, keep, hold), out...  52.8 us

profile of v3, /device:TPU:1, one launch (start us, length us, event | category | flops | bytes accessed | tf_op | source)
XLA Modules:
  0.0 53.7 jit_solution(13678932862332528243)
XLA Ops:
  0.0 52.8 %shard_map.55 = f32[5,256,128]{2,1,0:T(8,128)S(1)} custom-call(f32[5,256,128]{2,1,0:T(8,128)} %bitcast.5, f32[5,256,128]{2,1,0:T(8,128)} %bitcast.6, bf16[6,32,8,128]{3,2,1,0:T(8,128)(2,1)} %bitcast.7, f32[5,5]{1,0:T(8,128)} %coupling.1, f32[5,32]{1,0:T(8,128)} %prec.1), custom_call_target="tpu_custom_call" | custom-call | tf_op jit(solution)/shard_map/pallas_call | solution.py:538
  52.8 0.8 %copy.7 = f32[1,1,5,32,8,128]{5,4,3,2,1,0:T(8,128)} copy(f32[1,1,5,32,8,128]{5,4,3,2,1,0:T(8,128)S(1)} %bitcast.4) | data formatting | bytes 1310720

commit v4 on v3

--- a/solution.py
+++ b/solution.py
@@ -51,7 +51,7 @@
     prec_in = pltpu.make_async_copy(prec, ps, load.at[groups + steps + 1])
     coupling_in = pltpu.make_async_copy(coupling, cs, load.at[groups + steps + 2])
 
-    order = tuple(range(keep, groups)) + tuple(range(keep))
+    order = tuple(reversed(range(groups)))
     for g in order:
         state_in(g).start()
     coupling_in.start()
@@ -218,7 +218,7 @@
             copy.start()
 
     def over(a, b, f):
-        lax.fori_loop(a, b, lambda g, c: (f(g), c)[1], 0)
+        lax.fori_loop(a, b, lambda i, c: (f(a + b - 1 - i), c)[1], 0)
 
     for g in order:
         state_in(g).wait()
@@ -329,10 +329,10 @@
             fold(n + 1, g, packed)
             start(field_halo(n + 1, g, n + 2))
 
-    @functools.partial(over, 0, steps - 1)
-    def _(n):
+    def early_steps(n):
         over(lo, hi, lambda g: forward(n, g, False))
 
+    lax.fori_loop(0, steps - 1, lambda n, c: (early_steps(n), c)[1], 0)
     over(lo, hi, lambda g: forward(steps - 1, g, True))
 
     prec_in.wait()

time: 53.9 us -> 52.6 us (0.976)
  Pallas kernels: 52.8 us -> 51.7 us
    pallas_call x1, Pallas kernels: 52.8 us -> 51.7 us  [body(): pl.pallas_call(functools.partial(kernel, windows, tiles, keep, hold), out...]
where the time goes in v4:
time: 52.6 us; the launch traced here: 52.5 us
  Pallas kernels  51.7 us (98%)
  local copies, waits for them, and re-layouts  0.84 us (2%)
    pallas_call x1, Pallas kernels, body(): pl.pallas_call(functools.partial(kernel, windows, tiles, keep, hold), out...  51.7 us

profile of v4, /device:TPU:1, one launch (start us, length us, event | category | flops | bytes accessed | tf_op | source)
XLA Modules:
  0.0 52.5 jit_solution(12474130319895519123)
XLA Ops:
  0.0 51.7 %shard_map.55 = f32[5,256,128]{2,1,0:T(8,128)S(1)} custom-call(f32[5,256,128]{2,1,0:T(8,128)} %bitcast.5, f32[5,256,128]{2,1,0:T(8,128)} %bitcast.6, bf16[6,32,8,128]{3,2,1,0:T(8,128)(2,1)} %bitcast.7, f32[5,5]{1,0:T(8,128)} %coupling.1, f32[5,32]{1,0:T(8,128)} %prec.1), custom_call_target="tpu_custom_call" | custom-call | tf_op jit(solution)/shard_map/pallas_call | solution.py:538
  51.7 0.8 %copy.7 = f32[1,1,5,32,8,128]{5,4,3,2,1,0:T(8,128)} copy(f32[1,1,5,32,8,128]{5,4,3,2,1,0:T(8,128)S(1)} %bitcast.4) | data formatting | bytes 1310720

commit v5 on v4

--- a/solution.py
+++ b/solution.py
@@ -223,20 +223,21 @@
     for g in order:
         state_in(g).wait()
         convert_state(g)
-        if g == order[0]:
-            pl.semaphore_wait(barrier, met)
+        packed = pack_state(g, 0)
+        fold(0, g, packed)
+        yp[0, g] = packed
+    pl.semaphore_wait(barrier, met)
+    for g in order:
         if g >= keep:
             @when(lends)
             def _():
                 lend_state(g).start()
 
-        packed = pack_state(g, 0)
-        fold(0, g, packed)
-        yp[0, g] = packed
-
-        @when((k < end) & (g < hi))
-        def _():
-            start(field_halo(0, g, 0))
+    for part_of in (slice(0, 2), slice(2, 4)):
+        for g in order:
+            @when((k < end) & (g < hi))
+            def _():
+                start(field_halo(0, g, 0)[part_of])
 
     @when(k > 0)
     def _():

time: 52.6 us -> 51.8 us (0.985)
  Pallas kernels: 51.7 us -> 50.8 us
    pallas_call x1, Pallas kernels: 51.7 us -> 50.8 us  [body(): pl.pallas_call(functools.partial(kernel, windows, tiles, keep, hold), out...]
where the time goes in v5:
time: 51.8 us; the launch traced here: 51.7 us
  Pallas kernels  50.8 us (98%)
  local copies, waits for them, and re-layouts  0.84 us (2%)
    pallas_call x1, Pallas kernels, body(): pl.pallas_call(functools.partial(kernel, windows, tiles, keep, hold), out...  50.8 us

profile of v5, /device:TPU:1, one launch (start us, length us, event | category | flops | bytes accessed | tf_op | source)
XLA Modules:
  0.0 51.7 jit_solution(13554291011021818310)
XLA Ops:
  0.0 50.8 %shard_map.55 = f32[5,256,128]{2,1,0:T(8,128)S(1)} custom-call(f32[5,256,128]{2,1,0:T(8,128)} %bitcast.5, f32[5,256,128]{2,1,0:T(8,128)} %bitcast.6, bf16[6,32,8,128]{3,2,1,0:T(8,128)(2,1)} %bitcast.7, f32[5,5]{1,0:T(8,128)} %coupling.1, f32[5,32]{1,0:T(8,128)} %prec.1), custom_call_target="tpu_custom_call" | custom-call | tf_op jit(solution)/shard_map/pallas_call | solution.py:539
  50.8 0.8 %copy.7 = f32[1,1,5,32,8,128]{5,4,3,2,1,0:T(8,128)} copy(f32[1,1,5,32,8,128]{5,4,3,2,1,0:T(8,128)S(1)} %bitcast.4) | data formatting | bytes 1310720

commit v6 on v5

--- a/solution.py
+++ b/solution.py
@@ -391,7 +391,7 @@
 
     @when(k > 0)
     def _():
-        over(0, groups, mismatch)
+        over(0, groups, lambda i: mismatch(jnp.where((k == 2) & (i < hold), lax.rem(i + keep, hold), i)))
 
     @when(is_first)
     def _():
@@ -442,7 +442,39 @@
             start(flux_halo(i + 1, g))
 
     for i in range(steps - 1):
-        over(back_lo, back_hi, functools.partial(backward, i))
+        over(back_lo, back_hi, lambda j, i=i: backward(i, jnp.where(k == 1, lax.rem(j + keep, hold), j)))
+
+    def sent(copies):
+        for copy in copies:
+            copy.wait_send()
+
+    @functools.partial(over, lo, hi)
+    def _(g):
+        for n in range(steps):
+            sent(field_halo(n, g, 0))
+        sent(gap_halo(g))
+        onward(g).wait_send()
+
+    @when(k > 0)
+    def _():
+        @functools.partial(over, 0, groups)
+        def _(g):
+            sent(weighted_halo(g))
+            sent(state_edges(g))
+            back(g).wait_send()
+
+    @when(k < end)
+    def _():
+        over(0, groups, lambda g: sent(wind_edges(g)))
+
+    if helping:
+        @when(lends)
+        def _():
+            @functools.partial(over, keep, groups)
+            def _(g):
+                lend_state(g).wait_send()
+                for n in range(steps):
+                    lend_winds(n, g).wait_send()
 
     obs_in.wait()
 
@@ -454,7 +486,8 @@
                 out[v, rows, :] = own - ret[v, g, r] if has_next else own
 
     @functools.partial(over, back_lo, back_hi)
-    def _(g):
+    def _(j):
+        g = jnp.where(k == 1, lax.rem(j + keep, hold), j)
         backward(steps - 1, g)
 
         @when(~is_last)
@@ -479,47 +512,15 @@
                 give_back(g).wait_recv()
                 finish(g, True)
 
-    def sent(copies):
-        for copy in copies:
-            copy.wait_send()
-
-    @functools.partial(over, lo, hi)
-    def _(g):
-        for n in range(steps):
-            sent(field_halo(n, g, 0))
-        sent(gap_halo(g))
-        onward(g).wait_send()
-
     @functools.partial(over, back_lo, back_hi)
     def _(g):
         for i in range(1, steps):
             sent(flux_halo(i, g))
 
-    @when(k > 0)
-    def _():
-        @functools.partial(over, 0, groups)
-        def _(g):
-            sent(weighted_halo(g))
-            sent(state_edges(g))
-            back(g).wait_send()
-
-    @when(k < end)
-    def _():
-        over(0, groups, lambda g: sent(wind_edges(g)))
-
     if helping:
         @when(is_last)
         def _():
             over(hold, groups, lambda g: give_back(g).wait_send())
-
-    if helping:
-        @when(lends)
-        def _():
-            @functools.partial(over, keep, groups)
-            def _(g):
-                lend_state(g).wait_send()
-                for n in range(steps):
-                    lend_winds(n, g).wait_send()
 
 
 def solution(mesh):

time: 51.8 us -> 51.6 us (level)
  no operation moved by 1% of the time
where the time goes in v6:
time: 51.6 us; the launch traced here: 51.4 us
  Pallas kernels  50.5 us (98%)
  local copies, waits for them, and re-layouts  0.84 us (2%)
    pallas_call x1, Pallas kernels, body(): pl.pallas_call(functools.partial(kernel, windows, tiles, keep, hold), out...  50.5 us

profile of v6, /device:TPU:1, one launch (start us, length us, event | category | flops | bytes accessed | tf_op | source)
XLA Modules:
  0.0 51.4 jit_solution(472373013643825848)
XLA Ops:
  0.0 50.5 %shard_map.55 = f32[5,256,128]{2,1,0:T(8,128)S(1)} custom-call(f32[5,256,128]{2,1,0:T(8,128)} %bitcast.5, f32[5,256,128]{2,1,0:T(8,128)} %bitcast.6, bf16[6,32,8,128]{3,2,1,0:T(8,128)(2,1)} %bitcast.7, f32[5,5]{1,0:T(8,128)} %coupling.1, f32[5,32]{1,0:T(8,128)} %prec.1), custom_call_target="tpu_custom_call" | custom-call | tf_op jit(solution)/shard_map/pallas_call | solution.py:540
  50.5 0.8 %copy.7 = f32[1,1,5,32,8,128]{5,4,3,2,1,0:T(8,128)} copy(f32[1,1,5,32,8,128]{5,4,3,2,1,0:T(8,128)S(1)} %bitcast.4) | data formatting | bytes 1310720

commit v7 on v6

--- a/solution.py
+++ b/solution.py
@@ -428,7 +428,9 @@
                 for b in range(variables):
                     total = total + cs[b, v] * values[b]
                 if final:
+                    rows = rows_of(g, r)
                     ret[v, g, r] = total
+                    out[v, rows, :] = wgt[v, g, r] + onat[v, rows, :] * fld[0, v, g, r] - total
                     continue
                 gf[i + 1, v, g, r] = total
                 if r == 0:
@@ -490,9 +492,6 @@
         g = jnp.where(k == 1, lax.rem(j + keep, hold), j)
         backward(steps - 1, g)
 
-        @when(~is_last)
-        def _():
-            finish(g, True)
         if helping:
             @when(is_last)
             def _():

time: 51.6 us -> 51.6 us (level)
  no operation moved by 1% of the time
where the time goes in v7:
time: 51.6 us; the launch traced here: 51.4 us
  Pallas kernels  50.5 us (98%)
  local copies, waits for them, and re-layouts  0.84 us (2%)
    pallas_call x1, Pallas kernels, body(): pl.pallas_call(functools.partial(kernel, windows, tiles, keep, hold), out...  50.5 us

profile of v7, /device:TPU:1, one launch (start us, length us, event | category | flops | bytes accessed | tf_op | source)
XLA Modules:
  0.0 51.4 jit_solution(5324422643743292589)
XLA Ops:
  0.0 50.5 %shard_map.55 = f32[5,256,128]{2,1,0:T(8,128)S(1)} custom-call(f32[5,256,128]{2,1,0:T(8,128)} %bitcast.5, f32[5,256,128]{2,1,0:T(8,128)} %bitcast.6, bf16[6,32,8,128]{3,2,1,0:T(8,128)(2,1)} %bitcast.7, f32[5,5]{1,0:T(8,128)} %coupling.1, f32[5,32]{1,0:T(8,128)} %prec.1), custom_call_target="tpu_custom_call" | custom-call | tf_op jit(solution)/shard_map/pallas_call | solution.py:539
  50.6 0.8 %copy.7 = f32[1,1,5,32,8,128]{5,4,3,2,1,0:T(8,128)} copy(f32[1,1,5,32,8,128]{5,4,3,2,1,0:T(8,128)S(1)} %bitcast.4) | data formatting | bytes 1310720
